TPU v7x, 128 devices: a whole 4x4x4 slice. The times are simulated.
128 devices in a mesh: gx: 8 (over z, y_hi), gy: 16 (over y_lo, x, core).
Axes of the slice: x: 4, y: 4 (y_hi: 2, y_lo: 2; y = y_hi * 2 + y_lo), z: 4, core: 2. Of those that a mesh axis runs over, the one named last changes fastest.
Arguments:
- spectrum: float32 [2, 1024, 16384], P(None, ('gx', 'gy')), may hold values from -6 to 6
- parameters: float32 [2], replicated, may hold values from -1.5 to 1.5
Outputs:
- advanced: float32 [2, 1024, 16384], P(None, ('gx', 'gy'))
All inputs are finite; a program needn't handle non-finite values.
Results may differ from a plain program's by a relative error of at most 0.0003.
Values sent between devices are 32-bit elements; how exact they have to be, the bound alone decides.
A program may use at most 128 MiB of HBM per device.

v0:
```python
import itertools
import math
import random

import jax
import jax.numpy as jnp
import numpy as np
from jax import lax
from jax.experimental import pallas as pl
from jax.experimental.pallas import tpu as pltpu
from jax.sharding import PartitionSpec as P

MESH = pl.DeviceIdType.MESH
F32 = jnp.float32
BF16 = jnp.bfloat16

time_step = 0.1
spacing = 0.25
DEVICES = 128
ROWS = 1024
COLS = 16384
TOTAL = ROWS * COLS
NORM = 1.0 / math.sqrt(TOTAL)
LANES = 128

FULL, HALF, QUARTER, FIRST, SECOND, THIRD = 0, 2, 1, 3, 4, 5
WEIGHT, LAST = 0, 1


def offsets():
    every = [o for o in itertools.product(range(4), range(4), range(4), range(2)) if any(o)]
    random.Random(0).shuffle(every)
    return sorted(every, key=lambda o: -sum(min(v, 4 - v) for v in o[:3]))


OTHERS = offsets()


def split_host(table):
    high = table.astype(np.float32).astype(jnp.bfloat16)
    low = (table - high.astype(np.float64)).astype(np.float32).astype(jnp.bfloat16)
    return high, low


def left_table(sign, scale):
    index = np.arange(128)
    angle = 2.0 * np.pi * (np.outer(index, index) % 128) / 128
    cosine, sine = np.cos(angle) * scale, sign * np.sin(angle) * scale
    high, low = split_host(np.block([[cosine, -sine], [sine, cosine]]))
    return np.concatenate([high, high, low], axis=1)


def right_table(sign, scale):
    index = np.arange(128)
    angle = 2.0 * np.pi * (np.outer(index, index) % 128) / 128
    cosine, sine = np.cos(angle) * scale, sign * np.sin(angle) * scale
    high, low = split_host(np.block([[cosine, sine], [-sine, cosine]]))
    return np.concatenate([high, high, low], axis=0)


def inner_turns():
    index = np.arange(128)
    angle = 2.0 * np.pi * np.outer(index, index) / COLS
    return np.stack([np.cos(angle), np.sin(angle)]).astype(np.float32)


def times(a, b):
    return a[0] * b[0] - a[1] * b[1], a[0] * b[1] + a[1] * b[0]


def times_conj(a, b):
    return a[0] * b[0] + a[1] * b[1], a[1] * b[0] - a[0] * b[1]


def plus(a, b):
    return a[0] + b[0], a[1] + b[1]


def minus(a, b):
    return a[0] - b[0], a[1] - b[1]


def turn(a, sign):
    return (-a[1], a[0]) if sign > 0 else (a[1], -a[0])


def four(x, sign):
    s02, d02 = plus(x[0], x[2]), minus(x[0], x[2])
    s13, d13 = plus(x[1], x[3]), turn(minus(x[1], x[3]), sign)
    return [plus(s02, s13), plus(d02, d13), minus(s02, s13), minus(d02, d13)]


def eight(x, sign):
    even, odd = four(x[0::2], sign), four(x[1::2], sign)
    half = math.sqrt(0.5)
    odd[1] = plus(odd[1], turn(odd[1], sign))
    odd[1] = (odd[1][0] * half, odd[1][1] * half)
    odd[2] = turn(odd[2], sign)
    odd[3] = minus(turn(odd[3], sign), odd[3])
    odd[3] = (odd[3][0] * half, odd[3][1] * half)
    return [plus(even[k], odd[k]) for k in range(4)] + [minus(even[k], odd[k]) for k in range(4)]


def cos_sin_quarter(quarters):
    whole = jnp.floor(quarters + 0.5)
    return cos_sin_near((quarters - whole) * (math.pi / 2), whole)


def cos_sin_near(x, whole):
    square = x * x
    sine = 1.0 / 362880.0
    for factor in (-1.0 / 5040.0, 1.0 / 120.0, -1.0 / 6.0, 1.0):
        sine = sine * square + factor
    sine = sine * x
    cosine = -1.0 / 3628800.0
    for factor in (1.0 / 40320.0, -1.0 / 720.0, 1.0 / 24.0, -0.5, 1.0):
        cosine = cosine * square + factor
    quadrant = whole.astype(jnp.int32) & 3
    swap = (quadrant & 1) == 1
    first = jnp.where(swap, sine, cosine)
    second = jnp.where(swap, cosine, sine)
    first = jnp.where((quadrant == 1) | (quadrant == 2), -first, first)
    second = jnp.where(quadrant >= 2, -second, second)
    return first, second


def cos_sin(x):
    whole = jnp.floor(x * (2.0 / math.pi) + 0.5)
    near = x - whole * 1.5703125
    near = near - whole * 4.837512969970703e-4
    near = near - whole * 7.549789948768648e-8
    return cos_sin_near(near, whole)


def series(z, order):
    real = jnp.full_like(z[0], 1.0 / math.factorial(14 + order))
    imag = jnp.zeros_like(z[0])
    for degree in range(13, -1, -1):
        real, imag = times((real, imag), z)
        real = real + 1.0 / math.factorial(degree + order)
    return real, imag


def over(z):
    scale = 1.0 / (z[0] * z[0] + z[1] * z[1])
    return z[0] * scale, -z[1] * scale


def pick(inside, a, b):
    return jnp.where(inside, a[0], b[0]), jnp.where(inside, a[1], b[1])


def coefficient_block(rows, columns, dispersion):
    mode = rows * COLS + columns
    signed = jnp.where(mode < TOTAL // 2, mode, mode - TOTAL).astype(F32)
    wavenum = signed * (2.0 * math.pi / (TOTAL * spacing))
    square = wavenum * wavenum
    z = time_step * (1.0 - square), -(time_step * dispersion * square)
    half = 0.5 * z[0], 0.5 * z[1]
    growth = jnp.exp(half[0])
    cosine, sine = cos_sin(half[1])
    decay_half = growth * cosine, growth * sine
    decay_full = times(decay_half, decay_half)

    inside = z[0] * z[0] + z[1] * z[1] < 1.0
    inverse = over((jnp.where(inside, 1.0, z[0]), jnp.where(inside, 0.0, z[1])))
    direct_one = times((decay_full[0] - 1.0, decay_full[1]), inverse)
    direct_two = times((direct_one[0] - 1.0, direct_one[1]), inverse)
    direct_three = times((direct_two[0] - 0.5, direct_two[1]), inverse)
    near_three = series(z, 3)
    near_two = times(near_three, z)
    near_two = near_two[0] + 0.5, near_two[1]
    near_one = times(near_two, z)
    near_one = near_one[0] + 1.0, near_one[1]
    one = pick(inside, near_one, direct_one)
    two = pick(inside, near_two, direct_two)
    three = pick(inside, near_three, direct_three)

    inside = half[0] * half[0] + half[1] * half[1] < 1.0
    inverse = over((jnp.where(inside, 1.0, half[0]), jnp.where(inside, 0.0, half[1])))
    direct = times((decay_half[0] - 1.0, decay_half[1]), inverse)
    half_one = pick(inside, series(half, 1), direct)

    return {
        FULL: decay_full,
        QUARTER: decay_half,
        HALF: tuple(0.5 * time_step * p for p in half_one),
        FIRST: tuple(time_step * (p - 3.0 * q + 4.0 * r) for p, q, r in zip(one, two, three)),
        SECOND: tuple(2.0 * time_step * (q - 2.0 * r) for q, r in zip(two, three)),
        THIRD: tuple(time_step * (4.0 * r - q) for q, r in zip(two, three)),
    }


def split(x):
    high = x.astype(BF16)
    return high, (x - high.astype(F32)).astype(BF16)


def from_left(table_ref, real, imag):
    high, low = split(jnp.concatenate([real, imag], axis=0))
    stacked = jnp.concatenate([high, low, high], axis=0)
    out = jnp.dot(table_ref[...], stacked, preferred_element_type=F32)
    return out[:128], out[128:]


def from_right(table_ref, real, imag):
    high, low = split(jnp.concatenate([real, imag], axis=1))
    stacked = jnp.concatenate([high, low, high], axis=1)
    out = jnp.dot(stacked, table_ref[...], preferred_element_type=F32)
    return out[:, :128], out[:, 128:]


def kernel(
    par, x_hbm, li_hbm, lf_hbm, ri_hbm, rf_hbm, tw_hbm,
    o_hbm,
    xin, li, lf, ri, rf, tw, turns, ticks, coef, w, nbuf, lin, tmp, mid,
    sb1, rb1, sb2, rb2,
    load_sem, enter_sem, leave_sem, s1, r1, s2, r2,
):
    gx, gy = lax.axis_index("gx"), lax.axis_index("gy")
    me = gx * 16 + gy
    z, y, x, core = me // 32, lax.rem(me // 8, 4), lax.rem(me // 2, 4), lax.rem(me, 2)
    zs = [lax.rem(z + i, 4) * 2 for i in range(4)]
    yh = [lax.rem(y + i, 4) // 2 for i in range(4)]
    yl = [lax.rem(lax.rem(y + i, 4), 2) * 8 for i in range(4)]
    xs = [lax.rem(x + i, 4) * 2 for i in range(4)]
    cs = [core, 1 - core]

    def partners():
        for oz, oy, ox, oc in OTHERS:
            tx = zs[oz] + yh[oy]
            ty = yl[oy] + xs[ox] + cs[oc]
            yield tx * 16 + ty, {"gx": tx, "gy": ty}

    def tile(index):
        return pl.ds(pl.multiple_of(index * 8, 8), 8)

    def band(index):
        return pl.ds(pl.multiple_of(index * LANES, LANES), LANES)

    loads = [
        pltpu.make_async_copy(source, target, load_sem.at[i])
        for i, (source, target) in enumerate(
            [(x_hbm, xin), (li_hbm, li), (lf_hbm, lf), (ri_hbm, ri), (rf_hbm, rf), (tw_hbm, tw)]
        )
    ]
    for load in loads:
        load.start()

    barrier = pltpu.get_barrier_semaphore()
    for _, there in partners():
        pl.semaphore_signal(barrier, 1, device_id=there, device_id_type=MESH)
    pl.semaphore_wait(barrier, DEVICES - 1)

    loads[0].wait()
    for part in range(2):
        for other, there in partners():
            pltpu.make_async_remote_copy(
                xin.at[part, :, band(other)], w.at[part, tile(me)],
                enter_sem.at[0], enter_sem.at[1], device_id=there, device_id_type=MESH,
            ).start()
        w[part, tile(me), :] = xin[part, :, band(me)]

    dispersion, twist = par[0], par[1]
    lane = lax.broadcasted_iota(jnp.int32, (8, LANES), 1)
    sub = lax.broadcasted_iota(jnp.int32, (8, LANES), 0)
    columns = me * LANES + lane

    def table_step(i, carry):
        k, a = i // 16, lax.rem(i, 16) * 8 + sub
        at = tile(i)
        turns[0, at, :], turns[1, at, :] = cos_sin_quarter(
            ((8 * a + k) * columns).astype(F32) * (4.0 / TOTAL)
        )
        ticks[0, at, :], ticks[1, at, :] = cos_sin_quarter((a * k).astype(F32) * (4.0 / ROWS))
        return carry

    lax.fori_loop(0, 128, table_step, 0)

    def coefficient_step(i, carry):
        at = tile(i)
        block = coefficient_block(i * 8 + sub, columns, dispersion)
        for slot, value in block.items():
            coef[slot, 0, at, :] = value[0]
            coef[slot, 1, at, :] = value[1]
        return carry

    lax.fori_loop(0, 128, coefficient_step, 0)

    for load in loads[1:]:
        load.wait()
    both = w.at[:, pl.ds(0, (DEVICES - 1) * 8)]
    pltpu.make_async_copy(both, both, enter_sem.at[1]).wait()

    def pair(ref, at):
        return ref[0, at, :], ref[1, at, :]

    def stage(s, carry):
        def open_step(i, c):
            values = eight([pair(w, tile(16 * b + i)) for b in range(8)], 1.0)
            for k in range(8):
                value = times(values[k], pair(ticks, tile(16 * k + i))) if k else values[0]
                tmp[tile(i), k * LANES : (k + 1) * LANES] = value[0]
                tmp[tile(16 + i), k * LANES : (k + 1) * LANES] = value[1]
            return c

        lax.fori_loop(0, 16, open_step, 0)

        def out_step(g, c):
            for j in range(2):
                wide = pl.ds(pl.multiple_of(g * 512 + j * 256, 256), 256)
                real, imag = from_left(li, tmp[0:128, wide], tmp[128:256, wide])
                for h in range(2):
                    kk = 2 * j + h
                    at = pl.ds(pl.multiple_of((4 * g + kk) * 128, 128), 128)
                    cut = slice(h * LANES, (h + 1) * LANES)
                    value = times((real[:, cut], imag[:, cut]), pair(turns, at))
                    sb1[s, g, pl.ds(kk, 128, stride=8), :] = value[0]
                    sb1[s, g, pl.ds(4 + kk, 128, stride=8), :] = value[1]
            for other, there in partners():
                pltpu.make_async_remote_copy(
                    sb1.at[s, g, tile(other)], rb1.at[s, g, tile(me)],
                    s1.at[s, g], r1.at[s, g], device_id=there, device_id_type=MESH,
                ).start()
            rb1[s, g, tile(me), :] = sb1[s, g, tile(me), :]
            return c

        lax.fori_loop(0, 2, out_step, 0)

        def linear(body):
            lax.fori_loop(0, 128, lambda i, c: (body(tile(i)), c)[1], 0)

        def put(slot, at, value):
            lin[slot, 0, at, :] = value[0]
            lin[slot, 1, at, :] = value[1]

        @pl.when(s == 0)
        def _():
            def body(at):
                put(0, at, times(pair(coef.at[QUARTER], at), pair(w, at)))
                put(2, at, times(pair(coef.at[FULL], at), pair(w, at)))

            linear(body)

        @pl.when(s == 1)
        def _():
            def body(at):
                put(1, at, times(pair(coef.at[QUARTER], at), pair(w, at)))
                put(2, at, plus(pair(lin.at[2], at), times(pair(coef.at[FIRST], at), pair(nbuf.at[0], at))))

            linear(body)

        @pl.when(s >= 2)
        def _():
            def body(at):
                put(2, at, plus(pair(lin.at[2], at), times(pair(coef.at[SECOND], at), pair(nbuf.at[s - 1], at))))

            linear(body)

        def row_step(g, c):
            most = rb1.at[s, g, pl.ds(0, (DEVICES - 1) * 8)]
            pltpu.make_async_copy(most, most, r1.at[s, g]).wait()
            inner = tw[0], tw[1]
            for j in range(2):
                real = jnp.concatenate(
                    [rb1[s, g, pl.ds(2 * j + h, 128, stride=8), :] for h in range(2)], axis=1
                )
                imag = jnp.concatenate(
                    [rb1[s, g, pl.ds(4 + 2 * j + h, 128, stride=8), :] for h in range(2)], axis=1
                )
                real, imag = from_left(li, real, imag)
                halves = [
                    times((real[:, h * LANES : (h + 1) * LANES], imag[:, h * LANES : (h + 1) * LANES]), inner)
                    for h in range(2)
                ]
                real, imag = from_right(
                    ri,
                    jnp.concatenate([halves[0][0], halves[1][0]], axis=0),
                    jnp.concatenate([halves[0][1], halves[1][1]], axis=0),
                )
                size = -(real * real + imag * imag)
                real, imag = size * (real - twist * imag), size * (imag + twist * real)
                real, imag = from_right(rf, real, imag)
                halves = [
                    times_conj((real[h * 128 : (h + 1) * 128], imag[h * 128 : (h + 1) * 128]), inner)
                    for h in range(2)
                ]
                real, imag = from_left(
                    lf,
                    jnp.concatenate([halves[0][0], halves[1][0]], axis=1),
                    jnp.concatenate([halves[0][1], halves[1][1]], axis=1),
                )
                for h in range(2):
                    cut = slice(h * LANES, (h + 1) * LANES)
                    sb2[s, g, pl.ds(2 * j + h, 128, stride=8), :] = real[:, cut]
                    sb2[s, g, pl.ds(4 + 2 * j + h, 128, stride=8), :] = imag[:, cut]
            for other, there in partners():
                pltpu.make_async_remote_copy(
                    sb2.at[s, g, tile(other)], rb2.at[s, g, tile(me)],
                    s2.at[s, g], r2.at[s, g], device_id=there, device_id_type=MESH,
                ).start()
            rb2[s, g, tile(me), :] = sb2[s, g, tile(me), :]
            return c

        lax.fori_loop(0, 2, row_step, 0)

        def back_step(g, c):
            most = rb2.at[s, g, pl.ds(0, (DEVICES - 1) * 8)]
            pltpu.make_async_copy(most, most, r2.at[s, g]).wait()
            for j in range(2):
                halves = []
                for h in range(2):
                    kk = 2 * j + h
                    at = pl.ds(pl.multiple_of((4 * g + kk) * 128, 128), 128)
                    halves.append(
                        times_conj(
                            (
                                rb2[s, g, pl.ds(kk, 128, stride=8), :],
                                rb2[s, g, pl.ds(4 + kk, 128, stride=8), :],
                            ),
                            pair(turns, at),
                        )
                    )
                real, imag = from_left(
                    lf,
                    jnp.concatenate([halves[0][0], halves[1][0]], axis=1),
                    jnp.concatenate([halves[0][1], halves[1][1]], axis=1),
                )
                for h in range(2):
                    at = pl.ds(pl.multiple_of((4 * g + 2 * j + h) * 128, 128), 128)
                    cut = slice(h * LANES, (h + 1) * LANES)
                    mid[0, at, :] = real[:, cut]
                    mid[1, at, :] = imag[:, cut]
            return c

        lax.fori_loop(0, 2, back_step, 0)

        base = jnp.maximum(s - 1, 0)
        which = s // 3
        double = s == 2
        scale_new = jnp.where(double, 2.0, 1.0).astype(F32)
        scale_old = jnp.where(double, -1.0, 0.0).astype(F32)
        slot = HALF + which * (THIRD - HALF)

        def close_step(i, c):
            values = []
            for k in range(8):
                value = pair(mid, tile(16 * k + i))
                values.append(times_conj(value, pair(ticks, tile(16 * k + i))) if k else value)
            values = eight(values, -1.0)
            for b in range(8):
                at = tile(16 * b + i)
                new = values[b]
                nbuf[s, 0, at, :] = new[0]
                nbuf[s, 1, at, :] = new[1]
                old = pair(nbuf.at[0], at)
                mixed = (scale_new * new[0] + scale_old * old[0], scale_new * new[1] + scale_old * old[1])
                value = plus(pair(lin.at[base], at), times(pair(coef.at[slot], at), mixed))
                w[0, at, :] = value[0]
                w[1, at, :] = value[1]
            return c

        lax.fori_loop(0, 16, close_step, 0)
        return carry

    lax.fori_loop(0, 4, stage, 0)

    own = []
    for part in range(2):
        for other, there in partners():
            pltpu.make_async_remote_copy(
                w.at[part, tile(other)], o_hbm.at[part, :, band(me)],
                leave_sem.at[0], leave_sem.at[1], device_id=there, device_id_type=MESH,
            ).start()
        copy = pltpu.make_async_copy(w.at[part, tile(me)], o_hbm.at[part, :, band(me)], load_sem.at[part])
        copy.start()
        own.append(copy)

    pltpu.make_async_copy(both, both, enter_sem.at[0]).wait()

    def sent(s, carry):
        for g in range(2):
            for buffer, sem in ((sb1, s1), (sb2, s2)):
                most = buffer.at[s, g, pl.ds(0, (DEVICES - 1) * 8)]
                pltpu.make_async_copy(most, most, sem.at[s, g]).wait()
        return carry

    lax.fori_loop(0, 4, sent, 0)
    for copy in own:
        copy.wait()
    pltpu.make_async_copy(both, both, leave_sem.at[0]).wait()
    pltpu.make_async_copy(both, both, leave_sem.at[1]).wait()


def local(spectrum, parameters):
    hbm = pl.BlockSpec(memory_space=pl.ANY)
    field = (2, ROWS, LANES)
    return pl.pallas_call(
        kernel,
        name="etdrk4",
        out_shape=jax.ShapeDtypeStruct(spectrum.shape, F32),
        in_specs=[pl.BlockSpec(memory_space=pltpu.SMEM)] + [hbm] * 6,
        out_specs=hbm,
        scratch_shapes=[
            pltpu.VMEM(spectrum.shape, F32),
            pltpu.VMEM((256, 768), BF16),
            pltpu.VMEM((256, 768), BF16),
            pltpu.VMEM((768, 256), BF16),
            pltpu.VMEM((768, 256), BF16),
            pltpu.VMEM((2, 128, 128), F32),
            pltpu.VMEM(field, F32),
            pltpu.VMEM(field, F32),
            pltpu.VMEM((6,) + field, F32),
            pltpu.VMEM(field, F32),
            pltpu.VMEM((4,) + field, F32),
            pltpu.VMEM((3,) + field, F32),
            pltpu.VMEM((256, 1024), F32),
            pltpu.VMEM(field, F32),
        ]
        + [pltpu.VMEM((4, 2, 1024, LANES), F32)] * 4
        + [
            pltpu.SemaphoreType.DMA((6,)),
            pltpu.SemaphoreType.DMA((2,)),
            pltpu.SemaphoreType.DMA((2,)),
        ]
        + [pltpu.SemaphoreType.DMA((4, 2))] * 4,
        compiler_params=pltpu.CompilerParams(
            collective_id=0, has_side_effects=True, vmem_limit_bytes=60 * 1024 * 1024
        ),
    )(
        parameters,
        spectrum,
        jnp.asarray(left_table(1.0, 1.0)),
        jnp.asarray(left_table(-1.0, 1.0)),
        jnp.asarray(right_table(1.0, NORM)),
        jnp.asarray(right_table(-1.0, NORM)),
        jnp.asarray(inner_turns()),
    )


def solution(mesh):
    return jax.shard_map(
        local,
        mesh=mesh,
        in_specs=(P(None, ("gx", "gy"), None), P()),
        out_specs=P(None, ("gx", "gy"), None),
        check_vma=False,
    )
```

profile of v0, /device:TPU:1, one launch (start us, length us, event | category | flops | bytes accessed | tf_op | source)
XLA Modules:
  0.0 157.6 jit_solution(14134742301339563690)
XLA Ops:
  0.0 155.3 %etdrk4.1 = f32[2,8,16384]{2,1,0:T(8,128)} custom-call(f32[2]{0:T(128)} %par.1, f32[2,8,16384]{2,1,0:T(8,128)} %x_hbm.1, bf16[256,768]{1,0:T(8,128)(2,1)} %constant.10.clone.li_hbm, bf16[256,768]{1,0:T(8,128)(2,1)} %constant.11.clone.lf_hbm, bf16[768,256]{1,0:T(8,128)(2,1)} %constant.12.clone.ri_hbm, bf16[768,256]{1,0:T(8,128)(2,1)} %constant.13.clone.rf_hbm, ...), custom_call_target="tpu_custom_call" | custom-call | tf_op jit(solution)/shard_map/etdrk4/pallas_call | solution.py:498
  155.3 2.3 %copy.9 = f32[2,8,16384]{2,1,0:T(8,128)} copy(f32[2,8,16384]{2,1,0:T(8,128)} %etdrk4.1) | data formatting | bytes 2097152
where the time goes:
time: 158 us
  Pallas kernels  155 us (98%)
  local copies, waits for them, and re-layouts  2.26 us (1%)
    pallas_call x1, Pallas kernels, local(): pl.pallas_call(kernel, name='etdrk4', out_shape=jax.ShapeDtypeStruct(spec...  155 us

commit v1 on v0

v1 whole, which is shorter than its diff:
```python
import itertools
import math
import random

import jax
import jax.numpy as jnp
import numpy as np
from jax import lax
from jax.experimental import pallas as pl
from jax.experimental.pallas import tpu as pltpu
from jax.sharding import PartitionSpec as P

MESH = pl.DeviceIdType.MESH
F32 = jnp.float32
BF16 = jnp.bfloat16

time_step = 0.1
spacing = 0.25
DEVICES = 128
ROWS = 1024
COLS = 16384
TOTAL = ROWS * COLS
NORM = 1.0 / math.sqrt(TOTAL)
LANES = 128
PIECES = 4
STEP = 32

FULL, HALF, QUARTER, FIRST, SECOND, THIRD = 0, 2, 1, 3, 4, 5
WEIGHT, LAST = 0, 1


def offsets():
    every = [o for o in itertools.product(range(4), range(4), range(4), range(2)) if any(o)]
    random.Random(0).shuffle(every)
    every.sort(key=lambda o: -sum(min(v, 4 - v) for v in o[:3]))
    groups = {}
    for o in every:
        hop = next(((axis, o[axis]) for axis in (2, 1, 0) if o[axis]), None)
        groups.setdefault(hop, []).append(o)
    turns = itertools.zip_longest(*groups.values())
    return [o for turn in turns for o in turn if o is not None]


OTHERS = offsets()


def split_host(table):
    high = table.astype(np.float32).astype(jnp.bfloat16)
    low = (table - high.astype(np.float64)).astype(np.float32).astype(jnp.bfloat16)
    return high, low


def left_table(sign, scale):
    index = np.arange(128)
    angle = 2.0 * np.pi * (np.outer(index, index) % 128) / 128
    cosine, sine = np.cos(angle) * scale, sign * np.sin(angle) * scale
    high, low = split_host(np.block([[cosine, -sine], [sine, cosine]]))
    return np.concatenate([high, high, low], axis=1)


def right_table(sign, scale):
    index = np.arange(128)
    angle = 2.0 * np.pi * (np.outer(index, index) % 128) / 128
    cosine, sine = np.cos(angle) * scale, sign * np.sin(angle) * scale
    high, low = split_host(np.block([[cosine, sine], [-sine, cosine]]))
    return np.concatenate([high, high, low], axis=0)


def inner_turns():
    index = np.arange(128)
    angle = 2.0 * np.pi * np.outer(index, index) / COLS
    return np.stack([np.cos(angle), np.sin(angle)]).astype(np.float32)


def times(a, b):
    return a[0] * b[0] - a[1] * b[1], a[0] * b[1] + a[1] * b[0]


def times_conj(a, b):
    return a[0] * b[0] + a[1] * b[1], a[1] * b[0] - a[0] * b[1]


def plus(a, b):
    return a[0] + b[0], a[1] + b[1]


def minus(a, b):
    return a[0] - b[0], a[1] - b[1]


def turn(a, sign):
    return (-a[1], a[0]) if sign > 0 else (a[1], -a[0])


def four(x, sign):
    s02, d02 = plus(x[0], x[2]), minus(x[0], x[2])
    s13, d13 = plus(x[1], x[3]), turn(minus(x[1], x[3]), sign)
    return [plus(s02, s13), plus(d02, d13), minus(s02, s13), minus(d02, d13)]


def across(x, lower):
    return pltpu.roll(x, 64, 1) + jnp.where(lower, x, -x)


def swap(a, b, lower):
    return jnp.where(lower, a, pltpu.roll(b, 64, 1)), jnp.where(lower, pltpu.roll(a, 64, 1), b)


def eighth_turns(lower, sign):
    half = math.sqrt(0.5)
    return [
        (jnp.where(lower, 1.0, c), jnp.where(lower, 0.0, sign * v))
        for c, v in ((half, half), (0.0, 1.0), (-half, half))
    ]


def open_eight(x, lower):
    x = [(across(r, lower), across(i, lower)) for r, i in x]
    factors = eighth_turns(lower, 1.0)
    return four([x[0]] + [times(v, f) for v, f in zip(x[1:], factors)], 1.0)


def close_eight(x, lower):
    x = four(x, -1.0)
    factors = eighth_turns(lower, -1.0)
    x = [x[0]] + [times(v, f) for v, f in zip(x[1:], factors)]
    return [(across(r, lower), across(i, lower)) for r, i in x]


def cos_sin_quarter(quarters):
    whole = jnp.floor(quarters + 0.5)
    return cos_sin_near((quarters - whole) * (math.pi / 2), whole)


def cos_sin_near(x, whole):
    square = x * x
    sine = 1.0 / 362880.0
    for factor in (-1.0 / 5040.0, 1.0 / 120.0, -1.0 / 6.0, 1.0):
        sine = sine * square + factor
    sine = sine * x
    cosine = -1.0 / 3628800.0
    for factor in (1.0 / 40320.0, -1.0 / 720.0, 1.0 / 24.0, -0.5, 1.0):
        cosine = cosine * square + factor
    quadrant = whole.astype(jnp.int32) & 3
    swap = (quadrant & 1) == 1
    first = jnp.where(swap, sine, cosine)
    second = jnp.where(swap, cosine, sine)
    first = jnp.where((quadrant == 1) | (quadrant == 2), -first, first)
    second = jnp.where(quadrant >= 2, -second, second)
    return first, second


def cos_sin(x):
    whole = jnp.floor(x * (2.0 / math.pi) + 0.5)
    near = x - whole * 1.5703125
    near = near - whole * 4.837512969970703e-4
    near = near - whole * 7.549789948768648e-8
    return cos_sin_near(near, whole)


def series(z, order):
    real = jnp.full_like(z[0], 1.0 / math.factorial(14 + order))
    imag = jnp.zeros_like(z[0])
    for degree in range(13, -1, -1):
        real, imag = times((real, imag), z)
        real = real + 1.0 / math.factorial(degree + order)
    return real, imag


def over(z):
    scale = 1.0 / (z[0] * z[0] + z[1] * z[1])
    return z[0] * scale, -z[1] * scale


def pick(inside, a, b):
    return jnp.where(inside, a[0], b[0]), jnp.where(inside, a[1], b[1])


def coefficient_block(rows, columns, dispersion):
    mode = rows * COLS + columns
    signed = jnp.where(mode < TOTAL // 2, mode, mode - TOTAL).astype(F32)
    wavenum = signed * (2.0 * math.pi / (TOTAL * spacing))
    square = wavenum * wavenum
    z = time_step * (1.0 - square), -(time_step * dispersion * square)
    half = 0.5 * z[0], 0.5 * z[1]
    growth = jnp.exp(half[0])
    cosine, sine = cos_sin(half[1])
    decay_half = growth * cosine, growth * sine
    decay_full = times(decay_half, decay_half)

    inside = z[0] * z[0] + z[1] * z[1] < 1.0
    inverse = over((jnp.where(inside, 1.0, z[0]), jnp.where(inside, 0.0, z[1])))
    direct_one = times((decay_full[0] - 1.0, decay_full[1]), inverse)
    direct_two = times((direct_one[0] - 1.0, direct_one[1]), inverse)
    direct_three = times((direct_two[0] - 0.5, direct_two[1]), inverse)
    near_three = series(z, 3)
    near_two = times(near_three, z)
    near_two = near_two[0] + 0.5, near_two[1]
    near_one = times(near_two, z)
    near_one = near_one[0] + 1.0, near_one[1]
    one = pick(inside, near_one, direct_one)
    two = pick(inside, near_two, direct_two)
    three = pick(inside, near_three, direct_three)

    inside = half[0] * half[0] + half[1] * half[1] < 1.0
    inverse = over((jnp.where(inside, 1.0, half[0]), jnp.where(inside, 0.0, half[1])))
    direct = times((decay_half[0] - 1.0, decay_half[1]), inverse)
    half_one = pick(inside, series(half, 1), direct)

    return {
        FULL: decay_full,
        QUARTER: decay_half,
        HALF: tuple(0.5 * time_step * p for p in half_one),
        FIRST: tuple(time_step * (p - 3.0 * q + 4.0 * r) for p, q, r in zip(one, two, three)),
        SECOND: tuple(2.0 * time_step * (q - 2.0 * r) for q, r in zip(two, three)),
        THIRD: tuple(time_step * (4.0 * r - q) for q, r in zip(two, three)),
    }


def split(x):
    high = x.astype(BF16)
    return high, (x - high.astype(F32)).astype(BF16)


def from_left(table_ref, real, imag):
    high, low = split(jnp.concatenate([real, imag], axis=0))
    stacked = jnp.concatenate([high, low, high], axis=0)
    out = jnp.dot(table_ref[...], stacked, preferred_element_type=F32)
    return out[:128], out[128:]


def from_right(table_ref, real, imag):
    high, low = split(jnp.concatenate([real, imag], axis=1))
    stacked = jnp.concatenate([high, low, high], axis=1)
    out = jnp.dot(stacked, table_ref[...], preferred_element_type=F32)
    return out[:, :128], out[:, 128:]


def kernel(
    par, x_hbm, li_hbm, lf_hbm, ri_hbm, rf_hbm, tw_hbm,
    o_hbm,
    xin, packed, entered, li, lf, ri, rf, tw, turns, ticks, coef, w, nbuf, lin, tmp, mid, leaving,
    sb1, rb1, sb2, rb2,
    load_sem, enter_s, enter_r, leave_s, leave_r, s1, r1, s2, r2,
):
    gx, gy = lax.axis_index("gx"), lax.axis_index("gy")
    me = gx * 16 + gy
    z, y, x, core = me // 32, lax.rem(me // 8, 4), lax.rem(me // 2, 4), lax.rem(me, 2)
    zs = [lax.rem(z + i, 4) * 2 for i in range(4)]
    yh = [lax.rem(y + i, 4) // 2 for i in range(4)]
    yl = [lax.rem(lax.rem(y + i, 4), 2) * 8 for i in range(4)]
    xs = [lax.rem(x + i, 4) * 2 for i in range(4)]
    cs = [core, 1 - core]

    def partners():
        for oz, oy, ox, oc in OTHERS:
            tx = zs[oz] + yh[oy]
            ty = yl[oy] + xs[ox] + cs[oc]
            yield tx * 16 + ty, {"gx": tx, "gy": ty}

    def tile(index):
        return pl.ds(pl.multiple_of(index * 8, 8), 8)

    def half_tile(index, h):
        return pl.ds(pl.multiple_of(index * 8 + h * 4, 4), 4)

    def block(index):
        return pl.ds(pl.multiple_of(index * 128, 128), 128)

    def pair(ref, at):
        return ref[0, at, :], ref[1, at, :]

    def store(ref, at, value):
        ref[0, at, :] = value[0]
        ref[1, at, :] = value[1]

    def wait_for(ref, sem):
        pltpu.make_async_copy(ref, ref, sem).wait()

    def span(index, height):
        return pl.ds(pl.multiple_of(index, height), height)

    def loop(count, body, unroll=1):
        def step(i, carry):
            for j in range(unroll):
                body(i * unroll + j)
            return carry

        lax.fori_loop(0, count // unroll if unroll > 1 else count, step, 0)

    loads = [
        pltpu.make_async_copy(source, target, load_sem.at[i])
        for i, (source, target) in enumerate(
            [(x_hbm, xin), (li_hbm, li), (lf_hbm, lf), (ri_hbm, ri), (rf_hbm, rf), (tw_hbm, tw)]
        )
    ]
    loads[0].start()

    barrier = pltpu.get_barrier_semaphore()
    for _, there in partners():
        pl.semaphore_signal(barrier, 1, device_id=there, device_id_type=MESH)

    lane = lax.broadcasted_iota(jnp.int32, (8, LANES), 1)
    sub = lax.broadcasted_iota(jnp.int32, (8, LANES), 0)
    lower = lane < 64
    lower_tall = lax.broadcasted_iota(jnp.int32, (128, LANES), 1) < 64
    lower_step = lax.broadcasted_iota(jnp.int32, (STEP, LANES), 1) < 64
    upper_bit = lane // 64
    column = lax.rem(lane, 64)

    loads[0].wait()

    def pack(t):
        first, second = swap(xin[0, :, block(t)], xin[1, :, block(t)], lower)
        packed[0, tile(t), :] = first
        packed[1, tile(t), :] = second

    with jax.named_scope("pack"):
        loop(128, pack, 8)
    for load in loads[1:]:
        load.start()
    with jax.named_scope("greet"):
        pl.semaphore_wait(barrier, DEVICES - 1)

    def enter(h):
        for other, there in partners():
            pltpu.make_async_remote_copy(
                packed.at[h, tile(other)], entered.at[h, tile(me)],
                enter_s.at[h], enter_r.at[h], device_id=there, device_id_type=MESH,
            ).start()
        entered[h, tile(me), :] = packed[h, tile(me), :]

    with jax.named_scope("enter"):
        loop(2, enter)

    dispersion, twist = par[0], par[1]

    def turn_table(i):
        h, k, a = i // 64, lax.rem(i // 16, 4), lax.rem(i, 16) * 8 + sub
        number = (8 * a + 2 * k + upper_bit) * (me * LANES + 64 * h + column)
        store(turns.at[h], tile(lax.rem(i, 64)), cos_sin_quarter(number.astype(F32) * (4.0 / TOTAL)))

    with jax.named_scope("turn_table"):
        loop(128, turn_table, 4)

    def tick_table(i):
        number = (lax.rem(i, 16) * 8 + sub) * (2 * (i // 16) + upper_bit)
        store(ticks, tile(i), cos_sin_quarter(number.astype(F32) * (4.0 / ROWS)))

    with jax.named_scope("tick_table"):
        loop(64, tick_table, 4)


    def coefficient_table(h, i):
        at = tile(i)
        rows = i * 8 + sub + 512 * upper_bit
        for slot, value in coefficient_block(rows, me * LANES + 64 * h + column, dispersion).items():
            store(coef.at[slot, h], at, value)

    with jax.named_scope("coefs"):
        loop(64, lambda i: coefficient_table(0, i), 2)
    for load in loads[1:]:
        load.wait()

    def rows_of(digit, i):
        return span(digit * 128 + i * STEP, STEP)

    def open_rows(h, i, values):
        for k, value in enumerate(open_eight(values, lower_step)):
            value = times(value, pair(ticks, rows_of(k, i)))
            tmp[h, rows_of(0, i), k * LANES : (k + 1) * LANES] = value[0]
            tmp[h, rows_of(1, i), k * LANES : (k + 1) * LANES] = value[1]

    def closed_rows(h, i):
        values = [
            times_conj(pair(mid.at[h], rows_of(k, i)), pair(ticks, rows_of(k, i))) for k in range(4)
        ]
        return close_eight(values, lower_step)

    def back(s, g, h):
        with jax.named_scope("wait_back"):
            wait_for(rb2.at[s, g, pl.ds(0, (DEVICES - 1) * 4)], r2.at[s, g, h])
        values = []
        for k in range(2):
            value = (
                rb2[s, g, pl.ds(h * 4 + k, 128, stride=8), :],
                rb2[s, g, pl.ds(h * 4 + 2 + k, 128, stride=8), :],
            )
            values.append(times_conj(value, pair(turns.at[h], block(2 * g + k))))
        real, imag = from_left(
            lf,
            jnp.concatenate([values[0][0], values[1][0]], axis=1),
            jnp.concatenate([values[0][1], values[1][1]], axis=1),
        )
        for k in range(2):
            cut = slice(k * LANES, (k + 1) * LANES)
            store(mid.at[h], block(2 * g + k), (real[:, cut], imag[:, cut]))

    def stage(s, carry):
        def columns(h):
            @pl.when(s == 0)
            def _():
                with jax.named_scope("wait_enter"):
                    wait_for(entered.at[h, pl.ds(0, (DEVICES - 1) * 8)], enter_r.at[h])

                def body(i):
                    values = []
                    for b in range(4):
                        low = entered[h, rows_of(b, i), :]
                        high = entered[h, rows_of(b + 4, i), :]
                        values.append(swap(low, high, lower_step))
                    for b in range(4):
                        store(w.at[h], rows_of(b, i), values[b])
                    open_rows(h, i, values)

                with jax.named_scope("cols"):
                    loop(128 // STEP, body)

            @pl.when(s > 0)
            def _():
                with jax.named_scope("back1"):
                    back(s - 1, 1, h)

            @pl.when((s > 0) & (s < 4))
            def _():
                base = jnp.maximum(s - 2, 0)
                scale = jnp.where(s == 3, 2.0, 1.0).astype(F32)

                def body(i):
                    values = []
                    for b, new in enumerate(closed_rows(h, i)):
                        at = rows_of(b, i)
                        more = times(pair(coef.at[HALF, h], at), (scale * new[0], scale * new[1]))
                        values.append(plus(pair(lin.at[base, h], at), more))
                        store(nbuf.at[s - 1, h], at, new)
                        store(w.at[h], at, values[-1])
                    open_rows(h, i, values)

                with jax.named_scope("cols"):
                    loop(128 // STEP, body)

            @pl.when(s == 4)
            def _():
                def body(i):
                    for b, new in enumerate(closed_rows(h, i)):
                        at = rows_of(b, i)
                        value = plus(pair(lin.at[2, h], at), times(pair(coef.at[THIRD, h], at), new))
                        first, second = swap(value[0], value[1], lower_step)
                        leaving[h, at, :] = first
                        leaving[h, rows_of(b + 4, i), :] = second

                with jax.named_scope("cols"):
                    loop(128 // STEP, body)
                for other, there in partners():
                    pltpu.make_async_remote_copy(
                        leaving.at[h, tile(other)], o_hbm.at[h, tile(me)],
                        leave_s.at[h], leave_r.at[h], device_id=there, device_id_type=MESH,
                    ).start()
                pltpu.make_async_copy(leaving.at[h, tile(me)], o_hbm.at[h, tile(me)], load_sem.at[h]).start()

            @pl.when(s < 4)
            def _():
                def send(n):
                    half, g = lax.rem(h + n, 2), (n + 1) // 2
                    wide = pl.ds(pl.multiple_of(g * 256, 256), 256)
                    real, imag = from_left(li, tmp[half, 0:128, wide], tmp[half, 128:256, wide])
                    for k in range(2):
                        cut = slice(k * LANES, (k + 1) * LANES)
                        value = times((real[:, cut], imag[:, cut]), pair(turns.at[half], block(2 * g + k)))
                        sb1[s, g, pl.ds(half * 4 + k, 128, stride=8), :] = value[0]
                        sb1[s, g, pl.ds(half * 4 + 2 + k, 128, stride=8), :] = value[1]
                    for other, there in partners():
                        pltpu.make_async_remote_copy(
                            sb1.at[s, g, half_tile(other, half)], rb1.at[s, g, half_tile(me, half)],
                            s1.at[s, g], r1.at[s, g], device_id=there, device_id_type=MESH,
                        ).start()

                    @pl.when(half == 1)
                    def _():
                        rb1[s, g, tile(me), :] = sb1[s, g, tile(me), :]

                with jax.named_scope("sends1"):
                    loop(1 + 2 * h, send)

        loop(2, columns)

        def linear(body):
            def step(i):
                body(i // 16, span(lax.rem(i, 16) * 32, 32))

            with jax.named_scope("linear"):
                loop(32, step)

        def put(slot, h, at, value):
            store(lin.at[slot, h], at, value)

        @pl.when(s == 0)
        def _():
            with jax.named_scope("coefs1"):
                loop(64, lambda i: coefficient_table(1, i), 2)

            def body(h, at):
                value = pair(w.at[h], at)
                put(0, h, at, times(pair(coef.at[QUARTER, h], at), value))
                put(2, h, at, times(pair(coef.at[FULL, h], at), value))

            linear(body)

        @pl.when(s == 1)
        def _():
            def body(h, at):
                first = pair(nbuf.at[0, h], at)
                value = times(pair(coef.at[QUARTER, h], at), pair(w.at[h], at))
                less = times(pair(coef.at[HALF, h], at), first)
                more = plus(pair(lin.at[2, h], at), times(pair(coef.at[FIRST, h], at), first))
                put(1, h, at, minus(value, less))
                put(2, h, at, more)

            linear(body)

        @pl.when((s == 2) | (s == 3))
        def _():
            def body(h, at):
                more = times(pair(coef.at[SECOND, h], at), pair(nbuf.at[s - 1, h], at))
                put(2, h, at, plus(pair(lin.at[2, h], at), more))

            linear(body)

        def rows(g):
            with jax.named_scope("wait_rows"):
                wait_for(rb1.at[s, g, pl.ds(0, (DEVICES - 1) * 8)], r1.at[s, g])
            inner = tw[0], tw[1]

            def received(part, k):
                values = [
                    rb1[s, g, pl.ds(h * 4 + part * 2 + k, 128, stride=8), :] for h in range(2)
                ]
                return jnp.concatenate(swap(values[0], values[1], lower_tall), axis=1)

            for k in range(2):
                real, imag = from_left(li, received(0, k), received(1, k))
                parts = [
                    times((real[:, b * LANES : (b + 1) * LANES], imag[:, b * LANES : (b + 1) * LANES]), inner)
                    for b in range(2)
                ]
                real, imag = from_right(
                    ri,
                    jnp.concatenate([parts[0][0], parts[1][0]], axis=0),
                    jnp.concatenate([parts[0][1], parts[1][1]], axis=0),
                )
                size = -(real * real + imag * imag)
                real, imag = size * (real - twist * imag), size * (imag + twist * real)
                real, imag = from_right(rf, real, imag)
                parts = [
                    times_conj((real[b * 128 : (b + 1) * 128], imag[b * 128 : (b + 1) * 128]), inner)
                    for b in range(2)
                ]
                real, imag = from_left(
                    lf,
                    jnp.concatenate([parts[0][0], parts[1][0]], axis=1),
                    jnp.concatenate([parts[0][1], parts[1][1]], axis=1),
                )
                for part, value in enumerate((real, imag)):
                    for h, v in enumerate(swap(value[:, :LANES], value[:, LANES:], lower_tall)):
                        sb2[s, g, pl.ds(h * 4 + part * 2 + k, 128, stride=8), :] = v
            rb2[s, g, tile(me), :] = sb2[s, g, tile(me), :]

            def send(h):
                for other, there in partners():
                    pltpu.make_async_remote_copy(
                        sb2.at[s, g, half_tile(other, h)], rb2.at[s, g, half_tile(me, h)],
                        s2.at[s, g], r2.at[s, g, h], device_id=there, device_id_type=MESH,
                    ).start()

            with jax.named_scope("sends2"):
                loop(2, send)

        @pl.when(s < 4)
        def _():
            with jax.named_scope("rows"):
                loop(2, rows)
            with jax.named_scope("back0"):
                loop(2, lambda h: back(s, 0, h))

        return carry

    lax.fori_loop(0, 5, stage, 0)

    def sent(s):
        for g in range(2):
            for buffer, sem in ((sb1, s1), (sb2, s2)):
                wait_for(buffer.at[s, g, pl.ds(0, (DEVICES - 1) * 8)], sem.at[s, g])

    loop(4, sent)
    for h in range(2):
        most = packed.at[h, pl.ds(0, (DEVICES - 1) * 8)]
        wait_for(most, enter_s.at[h])
        wait_for(most, leave_s.at[h])
        pltpu.make_async_copy(leaving.at[h, tile(me)], o_hbm.at[h, tile(me)], load_sem.at[h]).wait()
        with jax.named_scope("wait_leave"):
            wait_for(most, leave_r.at[h])


def unpack_kernel(x_hbm, o_hbm, x_ref, o_ref, x_sem, o_sem):
    lower = lax.broadcasted_iota(jnp.int32, (8, LANES), 1) < 64
    tiles = DEVICES // PIECES
    into, out = [], []
    for i in range(PIECES):
        rows, lanes = pl.ds(i * tiles * 8, tiles * 8), pl.ds(i * tiles * LANES, tiles * LANES)
        into.append(pltpu.make_async_copy(x_hbm.at[:, rows], x_ref.at[:, rows], x_sem.at[i]))
        out.append(pltpu.make_async_copy(o_ref.at[:, :, lanes], o_hbm.at[:, :, lanes], o_sem.at[i]))
        into[-1].start()
    for i in range(PIECES):
        into[i].wait()
        for t in range(i * tiles, (i + 1) * tiles):
            at, lanes = slice(t * 8, t * 8 + 8), slice(t * LANES, t * LANES + LANES)
            o_ref[0, :, lanes], o_ref[1, :, lanes] = swap(x_ref[0, at, :], x_ref[1, at, :], lower)
        out[i].start()
    for copy in out:
        copy.wait()


def local(spectrum, parameters):
    hbm = pl.BlockSpec(memory_space=pl.ANY)
    field = (2, 2, ROWS // 2, LANES)
    whole = (2, ROWS, LANES)
    packed = pl.pallas_call(
        kernel,
        name="etdrk4",
        out_shape=jax.ShapeDtypeStruct(whole, F32),
        in_specs=[pl.BlockSpec(memory_space=pltpu.SMEM)] + [hbm] * 6,
        out_specs=hbm,
        scratch_shapes=[
            pltpu.VMEM(spectrum.shape, F32),
            pltpu.VMEM(whole, F32),
            pltpu.VMEM(whole, F32),
            pltpu.VMEM((256, 768), BF16),
            pltpu.VMEM((256, 768), BF16),
            pltpu.VMEM((768, 256), BF16),
            pltpu.VMEM((768, 256), BF16),
            pltpu.VMEM((2, 128, 128), F32),
            pltpu.VMEM(field, F32),
            pltpu.VMEM((2, ROWS // 2, LANES), F32),
            pltpu.VMEM((6,) + field, F32),
            pltpu.VMEM(field, F32),
            pltpu.VMEM((3,) + field, F32),
            pltpu.VMEM((3,) + field, F32),
            pltpu.VMEM((2, 256, 512), F32),
            pltpu.VMEM(field, F32),
            pltpu.VMEM(whole, F32),
        ]
        + [pltpu.VMEM((4, 2, ROWS, LANES), F32)] * 4
        + [pltpu.SemaphoreType.DMA((6,))]
        + [pltpu.SemaphoreType.DMA((2,))] * 4
        + [
            pltpu.SemaphoreType.DMA((4, 2)),
            pltpu.SemaphoreType.DMA((4, 2)),
            pltpu.SemaphoreType.DMA((4, 2)),
            pltpu.SemaphoreType.DMA((4, 2, 2)),
        ],
        compiler_params=pltpu.CompilerParams(
            collective_id=0, has_side_effects=True, vmem_limit_bytes=60 * 1024 * 1024
        ),
    )(
        parameters,
        spectrum,
        jnp.asarray(left_table(1.0, 1.0)),
        jnp.asarray(left_table(-1.0, 1.0)),
        jnp.asarray(right_table(1.0, NORM)),
        jnp.asarray(right_table(-1.0, NORM)),
        jnp.asarray(inner_turns()),
    )
    return pl.pallas_call(
        unpack_kernel,
        name="unpack",
        out_shape=jax.ShapeDtypeStruct(spectrum.shape, F32),
        in_specs=[hbm],
        out_specs=hbm,
        scratch_shapes=[
            pltpu.VMEM(whole, F32),
            pltpu.VMEM(spectrum.shape, F32),
            pltpu.SemaphoreType.DMA((PIECES,)),
            pltpu.SemaphoreType.DMA((PIECES,)),
        ],
        compiler_params=pltpu.CompilerParams(vmem_limit_bytes=60 * 1024 * 1024),
    )(packed)


def solution(mesh):
    return jax.shard_map(
        local,
        mesh=mesh,
        in_specs=(P(None, ("gx", "gy"), None), P()),
        out_specs=P(None, ("gx", "gy"), None),
        check_vma=False,
    )
```

time: 158 us -> 149 us (0.943)
  Pallas kernels: 155 us -> 149 us
  local copies, waits for them, and re-layouts: 2.26 us -> 0 us
    pallas_call x1 -> x2, Pallas kernels: 155 us -> 149 us  [the longest x1 147 us: local(): pl.pallas_call(kernel, name='etdrk4', out_shape=jax.ShapeDtypeStruct(whol...]
    unnamed x1 -> x0, local copies, waits for them, and re-layouts: 2.26 us -> none
where the time goes in v1:
time: 149 us
  Pallas kernels  149 us (100%)
    pallas_call x1, Pallas kernels, local(): pl.pallas_call(kernel, name='etdrk4', out_shape=jax.ShapeDtypeStruct(whol...  147 us

profile of v1, /device:TPU:1, one launch (start us, length us, event | category | flops | bytes accessed | tf_op | source)
XLA Modules:
  0.0 149.2 jit_solution(8949987048942968326)
XLA Ops:
  0.0 146.9 %etdrk4.1.x_hbm = f32[2,1024,128]{2,1,0:T(8,128)} custom-call(f32[2]{0:T(128)} %par.1, f32[2,8,16384]{2,1,0:T(8,128)} %x_hbm.1, bf16[256,768]{1,0:T(8,128)(2,1)} %constant.10.clone.li_hbm, bf16[256,768]{1,0:T(8,128)(2,1)} %constant.11.clone.lf_hbm, bf16[768,256]{1,0:T(8,128)(2,1)} %constant.12.clone.ri_hbm, bf16[768,256]{1,0:T(8,128)(2,1)} %constant.13.clone.rf_hbm, ...), custom_call_target="tpu_custom_call" | custom-call | tf_op jit(solution)/shard_map/etdrk4/pallas_call | solution.py:627
  147.0 2.3 %unpack.1 = f32[2,8,16384]{2,1,0:T(8,128)} custom-call(f32[2,1024,128]{2,1,0:T(8,128)} %etdrk4.1.x_hbm), custom_call_target="tpu_custom_call" | custom-call | tf_op jit(solution)/shard_map/unpack/pallas_call | solution.py:673

commit v2 on v1

--- a/solution.py
+++ b/solution.py
@@ -22,8 +22,9 @@
 TOTAL = ROWS * COLS
 NORM = 1.0 / math.sqrt(TOTAL)
 LANES = 128
+PACK = 16
 PIECES = 4
-STEP = 32
+STEP = 64
 
 FULL, HALF, QUARTER, FIRST, SECOND, THIRD = 0, 2, 1, 3, 4, 5
 WEIGHT, LAST = 0, 1
@@ -288,13 +289,13 @@
 
         lax.fori_loop(0, count // unroll if unroll > 1 else count, step, 0)
 
-    loads = [
-        pltpu.make_async_copy(source, target, load_sem.at[i])
-        for i, (source, target) in enumerate(
-            [(x_hbm, xin), (li_hbm, li), (lf_hbm, lf), (ri_hbm, ri), (rf_hbm, rf), (tw_hbm, tw)]
-        )
-    ]
-    loads[0].start()
+    loads = []
+    for i in range(PIECES):
+        lanes = pl.ds(i * COLS // PIECES, COLS // PIECES)
+        loads.append(pltpu.make_async_copy(x_hbm.at[:, :, lanes], xin.at[:, :, lanes], load_sem.at[i]))
+        loads[i].start()
+    for source, target in ((li_hbm, li), (lf_hbm, lf), (ri_hbm, ri), (rf_hbm, rf), (tw_hbm, tw)):
+        loads.append(pltpu.make_async_copy(source, target, load_sem.at[len(loads)]))
 
     barrier = pltpu.get_barrier_semaphore()
     for _, there in partners():
@@ -308,16 +309,17 @@
     upper_bit = lane // 64
     column = lax.rem(lane, 64)
 
-    loads[0].wait()
-
     def pack(t):
         first, second = swap(xin[0, :, block(t)], xin[1, :, block(t)], lower)
         packed[0, tile(t), :] = first
         packed[1, tile(t), :] = second
 
     with jax.named_scope("pack"):
-        loop(128, pack, 8)
-    for load in loads[1:]:
+        for i in range(PIECES):
+            loads[i].wait()
+            first = i * 128 // PIECES
+            loop(128 // PIECES, lambda t: pack(first + t), PACK)
+    for load in loads[PIECES:]:
         load.start()
     with jax.named_scope("greet"):
         pl.semaphore_wait(barrier, DEVICES - 1)
@@ -359,7 +361,7 @@
 
     with jax.named_scope("coefs"):
         loop(64, lambda i: coefficient_table(0, i), 2)
-    for load in loads[1:]:
+    for load in loads[PIECES:]:
         load.wait()
 
     def rows_of(digit, i):
@@ -397,6 +399,37 @@
             store(mid.at[h], block(2 * g + k), (real[:, cut], imag[:, cut]))
 
     def stage(s, carry):
+        def linear(body):
+            def step(i):
+                body(i // 16, span(lax.rem(i, 16) * 32, 32))
+
+            with jax.named_scope("linear"):
+                loop(32, step)
+
+        def put(slot, h, at, value):
+            store(lin.at[slot, h], at, value)
+
+        def linear_parts():
+            @pl.when(s == 1)
+            def _():
+                def body(h, at):
+                    first = pair(nbuf.at[0, h], at)
+                    value = times(pair(coef.at[QUARTER, h], at), pair(w.at[h], at))
+                    less = times(pair(coef.at[HALF, h], at), first)
+                    more = plus(pair(lin.at[2, h], at), times(pair(coef.at[FIRST, h], at), first))
+                    put(1, h, at, minus(value, less))
+                    put(2, h, at, more)
+
+                linear(body)
+
+            @pl.when((s == 2) | (s == 3))
+            def _():
+                def body(h, at):
+                    more = times(pair(coef.at[SECOND, h], at), pair(nbuf.at[s - 1, h], at))
+                    put(2, h, at, plus(pair(lin.at[2, h], at), more))
+
+                linear(body)
+
         def columns(h):
             @pl.when(s == 0)
             def _():
@@ -462,6 +495,11 @@
             def _():
                 def send(n):
                     half, g = lax.rem(h + n, 2), (n + 1) // 2
+
+                    @pl.when(n == 1)
+                    def _():
+                        linear_parts()
+
                     wide = pl.ds(pl.multiple_of(g * 256, 256), 256)
                     real, imag = from_left(li, tmp[half, 0:128, wide], tmp[half, 128:256, wide])
                     for k in range(2):
@@ -484,16 +522,6 @@
 
         loop(2, columns)
 
-        def linear(body):
-            def step(i):
-                body(i // 16, span(lax.rem(i, 16) * 32, 32))
-
-            with jax.named_scope("linear"):
-                loop(32, step)
-
-        def put(slot, h, at, value):
-            store(lin.at[slot, h], at, value)
-
         @pl.when(s == 0)
         def _():
             with jax.named_scope("coefs1"):
@@ -503,26 +531,6 @@
                 value = pair(w.at[h], at)
                 put(0, h, at, times(pair(coef.at[QUARTER, h], at), value))
                 put(2, h, at, times(pair(coef.at[FULL, h], at), value))
-
-            linear(body)
-
-        @pl.when(s == 1)
-        def _():
-            def body(h, at):
-                first = pair(nbuf.at[0, h], at)
-                value = times(pair(coef.at[QUARTER, h], at), pair(w.at[h], at))
-                less = times(pair(coef.at[HALF, h], at), first)
-                more = plus(pair(lin.at[2, h], at), times(pair(coef.at[FIRST, h], at), first))
-                put(1, h, at, minus(value, less))
-                put(2, h, at, more)
-
-            linear(body)
-
-        @pl.when((s == 2) | (s == 3))
-        def _():
-            def body(h, at):
-                more = times(pair(coef.at[SECOND, h], at), pair(nbuf.at[s - 1, h], at))
-                put(2, h, at, plus(pair(lin.at[2, h], at), more))
 
             linear(body)
 
@@ -650,7 +658,7 @@
             pltpu.VMEM(whole, F32),
         ]
         + [pltpu.VMEM((4, 2, ROWS, LANES), F32)] * 4
-        + [pltpu.SemaphoreType.DMA((6,))]
+        + [pltpu.SemaphoreType.DMA((PIECES + 5,))]
         + [pltpu.SemaphoreType.DMA((2,))] * 4
         + [
             pltpu.SemaphoreType.DMA((4, 2)),

time: 149 us -> 146 us (0.980)
  Pallas kernels: 149 us -> 146 us
    pallas_call x1, Pallas kernels: 147 us -> 143 us  [local(): pl.pallas_call(kernel, name='etdrk4', out_shape=jax.ShapeDtypeStruct(whol...]
where the time goes in v2:
time: 146 us
  Pallas kernels  146 us (100%)
    pallas_call x1, Pallas kernels, local(): pl.pallas_call(kernel, name='etdrk4', out_shape=jax.ShapeDtypeStruct(whol...  143 us

profile of v2, /device:TPU:1, one launch (start us, length us, event | category | flops | bytes accessed | tf_op | source)
XLA Modules:
  0.0 145.6 jit_solution(12788925512003849688)
XLA Ops:
  0.0 143.3 %etdrk4.1.x_hbm = f32[2,1024,128]{2,1,0:T(8,128)} custom-call(f32[2]{0:T(128)} %par.1, f32[2,8,16384]{2,1,0:T(8,128)} %x_hbm.1, bf16[256,768]{1,0:T(8,128)(2,1)} %constant.10.clone.li_hbm, bf16[256,768]{1,0:T(8,128)(2,1)} %constant.11.clone.lf_hbm, bf16[768,256]{1,0:T(8,128)(2,1)} %constant.12.clone.ri_hbm, bf16[768,256]{1,0:T(8,128)(2,1)} %constant.13.clone.rf_hbm, ...), custom_call_target="tpu_custom_call" | custom-call | tf_op jit(solution)/shard_map/etdrk4/pallas_call | solution.py:635
  143.3 2.3 %unpack.1 = f32[2,8,16384]{2,1,0:T(8,128)} custom-call(f32[2,1024,128]{2,1,0:T(8,128)} %etdrk4.1.x_hbm), custom_call_target="tpu_custom_call" | custom-call | tf_op jit(solution)/shard_map/unpack/pallas_call | solution.py:681

commit v3 on v2

--- a/solution.py
+++ b/solution.py
@@ -1,6 +1,5 @@
 import itertools
 import math
-import random
 
 import jax
 import jax.numpy as jnp
@@ -32,7 +31,6 @@
 
 def offsets():
     every = [o for o in itertools.product(range(4), range(4), range(4), range(2)) if any(o)]
-    random.Random(0).shuffle(every)
     every.sort(key=lambda o: -sum(min(v, 4 - v) for v in o[:3]))
     groups = {}
     for o in every:
@@ -545,31 +543,36 @@
                 ]
                 return jnp.concatenate(swap(values[0], values[1], lower_tall), axis=1)
 
+            real, imag = from_left(
+                li,
+                jnp.concatenate([received(0, 0), received(0, 1)], axis=1),
+                jnp.concatenate([received(1, 0), received(1, 1)], axis=1),
+            )
+            parts = [
+                times((real[:, b * LANES : (b + 1) * LANES], imag[:, b * LANES : (b + 1) * LANES]), inner)
+                for b in range(4)
+            ]
+            real, imag = from_right(
+                ri,
+                jnp.concatenate([p[0] for p in parts], axis=0),
+                jnp.concatenate([p[1] for p in parts], axis=0),
+            )
+            size = -(real * real + imag * imag)
+            real, imag = size * (real - twist * imag), size * (imag + twist * real)
+            real, imag = from_right(rf, real, imag)
+            parts = [
+                times_conj((real[b * 128 : (b + 1) * 128], imag[b * 128 : (b + 1) * 128]), inner)
+                for b in range(4)
+            ]
+            real, imag = from_left(
+                lf,
+                jnp.concatenate([p[0] for p in parts], axis=1),
+                jnp.concatenate([p[1] for p in parts], axis=1),
+            )
             for k in range(2):
-                real, imag = from_left(li, received(0, k), received(1, k))
-                parts = [
-                    times((real[:, b * LANES : (b + 1) * LANES], imag[:, b * LANES : (b + 1) * LANES]), inner)
-                    for b in range(2)
-                ]
-                real, imag = from_right(
-                    ri,
-                    jnp.concatenate([parts[0][0], parts[1][0]], axis=0),
-                    jnp.concatenate([parts[0][1], parts[1][1]], axis=0),
-                )
-                size = -(real * real + imag * imag)
-                real, imag = size * (real - twist * imag), size * (imag + twist * real)
-                real, imag = from_right(rf, real, imag)
-                parts = [
-                    times_conj((real[b * 128 : (b + 1) * 128], imag[b * 128 : (b + 1) * 128]), inner)
-                    for b in range(2)
-                ]
-                real, imag = from_left(
-                    lf,
-                    jnp.concatenate([parts[0][0], parts[1][0]], axis=1),
-                    jnp.concatenate([parts[0][1], parts[1][1]], axis=1),
-                )
                 for part, value in enumerate((real, imag)):
-                    for h, v in enumerate(swap(value[:, :LANES], value[:, LANES:], lower_tall)):
+                    low, high = value[:, 2 * k * LANES : (2 * k + 1) * LANES], value[:, (2 * k + 1) * LANES : (2 * k + 2) * LANES]
+                    for h, v in enumerate(swap(low, high, lower_tall)):
                         sb2[s, g, pl.ds(h * 4 + part * 2 + k, 128, stride=8), :] = v
             rb2[s, g, tile(me), :] = sb2[s, g, tile(me), :]
 

time: 146 us -> 143 us (0.979)
  Pallas kernels: 146 us -> 142 us
    pallas_call x1, Pallas kernels: 143 us -> 140 us  [local(): pl.pallas_call(kernel, name='etdrk4', out_shape=jax.ShapeDtypeStruct(whol...]
where the time goes in v3:
time: 143 us; the launch traced here: 142 us
  Pallas kernels  142 us (99%)
    pallas_call x1, Pallas kernels, local(): pl.pallas_call(kernel, name='etdrk4', out_shape=jax.ShapeDtypeStruct(whol...  140 us

profile of v3, /device:TPU:1, one launch (start us, length us, event | category | flops | bytes accessed | tf_op | source)
XLA Modules:
  0.0 142.4 jit_solution(5350294986065182511)
XLA Ops:
  0.0 140.2 %etdrk4.1.x_hbm = f32[2,1024,128]{2,1,0:T(8,128)} custom-call(f32[2]{0:T(128)} %par.1, f32[2,8,16384]{2,1,0:T(8,128)} %x_hbm.1, bf16[256,768]{1,0:T(8,128)(2,1)} %constant.10.clone.li_hbm, bf16[256,768]{1,0:T(8,128)(2,1)} %constant.11.clone.lf_hbm, bf16[768,256]{1,0:T(8,128)(2,1)} %constant.12.clone.ri_hbm, bf16[768,256]{1,0:T(8,128)(2,1)} %constant.13.clone.rf_hbm, ...), custom_call_target="tpu_custom_call" | custom-call | tf_op jit(solution)/shard_map/etdrk4/pallas_call | solution.py:638
  140.2 2.3 %unpack.1 = f32[2,8,16384]{2,1,0:T(8,128)} custom-call(f32[2,1024,128]{2,1,0:T(8,128)} %etdrk4.1.x_hbm), custom_call_target="tpu_custom_call" | custom-call | tf_op jit(solution)/shard_map/unpack/pallas_call | solution.py:684
